TPU v7x, 32 devices: a whole 2x2x4 slice. The times are simulated.
32 devices in a mesh: clips: 2 (over x), seq: 16 (over z, y, core).
Axes of the slice: x: 2, y: 2, z: 4, core: 2. Of those that a mesh axis runs over, the one named last changes fastest.
Arguments:
- video_q: bfloat16 [4096, 1536], P(('clips', 'seq')), parts along dimension 0, may hold values from -200 to 200
- video_k: bfloat16 [4096, 1536], P(('clips', 'seq')), parts along dimension 0, may hold values from -7 to 7
- video_v: bfloat16 [4096, 1536], P(('clips', 'seq')), parts along dimension 0, may hold values from -6 to 6
- audio_q: bfloat16 [256, 1536], P(('clips', 'seq')), parts along dimension 0, may hold values from -200 to 200
- audio_k: bfloat16 [256, 1536], P(('clips', 'seq')), parts along dimension 0, may hold values from -6 to 6
- audio_v: bfloat16 [256, 1536], P(('clips', 'seq')), parts along dimension 0, may hold values from -6 to 6
- radius: int32 [32], P(('clips', 'seq')), parts along dimension 0, may hold values from 1 to 2
- tile_list: int32 [32, 5], P('clips'), parts along dimension 0, may hold values from -1 to 15, as said below
- tile_count: int32 [32], P('clips'), parts along dimension 0, may hold values from 1 to 5, as said below
- video_gain: float32 [1536], replicated, may hold values from 0.5 to 1.5
- audio_gain: float32 [1536], replicated, may hold values from 0.5 to 1.5
Outputs:
- video_out: bfloat16 [4096, 1536], P(('clips', 'seq')), parts along dimension 0
- audio_out: bfloat16 [256, 1536], P(('clips', 'seq')), parts along dimension 0
There are 2 independent parts, one for each index of `clips`. A program takes and returns all parts, laid end to end along the dimension named above; an argument that names none is the same for every part. Nothing has to cross between parts.
Inputs may be any that keep to these rules, and one draw needn't show every extreme that they name: `tile_list`: row b names tile b first, then tile_count[b] - 1 distinct other tiles within 4 of b; the remaining entries are -1. `tile_count`: some block lists 5 tiles.
All inputs are finite; a program needn't handle non-finite values.
Results may differ from a plain program's by a relative error of at most 0.014.
Values may be sent and summed in bfloat16 or wider, within the bound.
A program may use at most 64 MiB of HBM per device.

v0:
```python
import functools

import jax
import jax.numpy as jnp
from jax import lax
from jax.experimental import pallas as pl
from jax.experimental.pallas import tpu as pltpu
from jax.sharding import PartitionSpec as P

HD = 128
RMAX = 2
SPAN = 4
LOG2E = 1.4426950408889634
SCALE = HD ** (-0.5) * LOG2E
NEG = -1e30
EPS = 1e-6
MESH = pl.DeviceIdType.MESH
LAG_Z = 2
LAG_C = 3
WINDOW = 4
AUDIO_PASS = 6
AUDIO_READY = 7


def kernel(
    n, heads, tok, aud, lmax,
    radius, tile_list, tile_count,
    vq_hbm, vk_hbm, vv_hbm, aq_hbm, ak_hbm, av_hbm, vgain_hbm, again_hbm,
    vout, aout,
    kv, audio, qown, aqown, aqin, qx, qr, part_o, part_s, back_o, back_s, attn, aattn, vgain, again,
    load_sem, own_sem, s_dk, r_dk, s_y, r_y, s_z, r_z, s_dy, r_dy, s_dz, r_dz,
    s_up, s_dn, s_ya, r_aud, s_daud, r_daud, s_q, r_q, s_bo, r_bo, s_bs, r_bs,
):
    me = lax.axis_index("seq")
    chips = n // 2
    chip = me // 2
    core = me % 2
    mate = chip * 2 + (1 - core)
    odd = chip % 2
    across_chip = chip + 1 - 2 * odd
    across = across_chip * 2 + core
    step = 2 - 4 * odd
    fwd_chip = chip + step
    has_fwd = (fwd_chip >= 0) & (fwd_chip < chips)
    src_chip = chip - step
    has_src = (src_chip >= 0) & (src_chip < chips)
    zchip = chip - 1 + 2 * odd
    fwd = jnp.clip(fwd_chip, 0, chips - 1) * 2 + core

    barrier = pltpu.get_barrier_semaphore()

    def greet(device):
        pl.semaphore_signal(barrier, inc=1, device_id={"seq": device}, device_id_type=MESH)

    low, high = chip >= 2, chip + 2 < chips
    greet(across)
    greet(mate)
    for exists, far_chip in ((high, chip + 2), (low, chip - 2)):
        @pl.when(exists)
        def _(far_chip=far_chip):
            greet(jnp.clip(far_chip, 0, chips - 1) * 2)
            greet(jnp.clip(far_chip, 0, chips - 1) * 2 + 1)

    loads = [
        pltpu.make_async_copy(aq_hbm, aqown, load_sem.at[0]),
        pltpu.make_async_copy(ak_hbm, audio.at[me, 0], load_sem.at[1]),
        pltpu.make_async_copy(av_hbm, audio.at[me, 1], load_sem.at[2]),
        pltpu.make_async_copy(vq_hbm, qown, load_sem.at[3]),
        pltpu.make_async_copy(vgain_hbm, vgain, load_sem.at[4]),
        pltpu.make_async_copy(again_hbm, again, load_sem.at[5]),
    ]

    def cols(h):
        return pl.ds(pl.multiple_of(h * HD, HD), HD)

    def own_head(h):
        return [
            pltpu.make_async_copy(side.at[:, cols(h)], kv.at[h, j, pl.ds(0, tok)], own_sem.at[h, j])
            for j, side in enumerate((vk_hbm, vv_hbm))
        ]

    for load in loads[:3]:
        load.start()

    def load_own(h, _):
        for load in own_head(h):
            load.start()
        return 0

    lax.fori_loop(0, heads, load_own, 0)
    for load in loads[3:]:
        load.start()
    @pl.when(jnp.logical_not(has_src))
    def _():
        def clear(h, _):
            kv[h, :, pl.ds(4 * tok, 2 * tok), :] = jnp.zeros((2, 2 * tok, HD), kv.dtype)
            return 0

        lax.fori_loop(0, heads, clear, 0)

    far = []
    for slot in range(4):
        far_chip = chip + (2 if slot < 2 else -2)
        exists = (far_chip >= 0) & (far_chip < chips)
        device = jnp.clip(far_chip, 0, chips - 1) * 2 + slot % 2
        there = (2 if slot < 2 else 0) + core
        far.append((slot, exists, device, there))

        @pl.when(jnp.logical_not(exists))
        def _(slot=slot):
            aqin[slot] = jnp.zeros(aqin.shape[1:], aqin.dtype)
            back_o[slot] = jnp.zeros(back_o.shape[1:], back_o.dtype)
            back_s[slot] = jnp.zeros(back_s.shape[1:], back_s.dtype)

    pl.semaphore_wait(barrier, 2 + 2 * high.astype(jnp.int32) + 2 * low.astype(jnp.int32))

    def remote(src, dst, s, r, device):
        return pltpu.make_async_remote_copy(
            src_ref=src, dst_ref=dst, send_sem=s, recv_sem=r,
            device_id={"seq": device}, device_id_type=MESH)

    def q_copy(slot, device, there):
        return remote(aqown, aqin.at[there], s_q.at[slot], r_q.at[there], device)

    def q_arrival(slot):
        return remote(aqown, aqin.at[slot], s_q.at[slot], r_q.at[slot], mate)

    loads[0].wait()
    for slot, exists, device, there in far:
        @pl.when(exists)
        def _(slot=slot, device=device, there=there):
            q_copy(slot, device, there).start()
    loads[1].wait()
    loads[2].wait()

    row, rows_all = chip // 2, chips // 2
    up_to = jnp.clip(chip + 2, 0, chips - 1) * 2 + core
    down_to = jnp.clip(chip - 2, 0, chips - 1) * 2 + core

    def aud_copy(sems, block, device):
        return remote(audio.at[block], audio.at[block], sems.at[block], r_aud.at[block], device)

    def daud_copy(block):
        return remote(audio.at[block], audio.at[block], s_daud.at[block], r_daud.at[block], mate)

    def spread_up(block):
        return aud_copy(s_up, block, up_to)

    def spread_down(block):
        return aud_copy(s_dn, block, down_to)

    def spread_across(block):
        return aud_copy(s_ya, block, across)

    def from_below(d, act):
        @pl.when(row - d >= 0)
        def _():
            block = jnp.maximum(me - 4 * d, 0)
            act(block)

    def from_above(d, act):
        @pl.when(row + d < rows_all)
        def _():
            block = jnp.minimum(me + 4 * d, n - 1)
            act(block)

    @pl.when(high)
    def _():
        spread_up(me).start()

    @pl.when(low)
    def _():
        spread_down(me).start()

    def column_step(d):
        def below(block):
            spread_up(block).wait_recv()

            @pl.when(high)
            def _():
                spread_up(block).start()
            spread_across(block).start()
            daud_copy(block).start()

        def above(block):
            spread_down(block).wait_recv()

            @pl.when(low)
            def _():
                spread_down(block).start()
            spread_across(block).start()
            daud_copy(block).start()

        from_below(d, below)
        from_above(d, above)

    def pass_audio(i, _):
        block = 4 * i + across % 4
        spread_across(block).wait_recv()
        daud_copy(block).start()
        return 0

    def take_audio(i, _):
        daud_copy(2 * i + 1 - core).wait_recv()
        return 0

    def kv_head(slot, h):
        return kv.at[h, :, pl.ds(slot * tok, tok)]

    def y_copy(h):
        return remote(kv_head(0, h), kv_head(2, h), s_y.at[h], r_y.at[h], across)

    def z_copy(h):
        return remote(kv_head(2, h), kv_head(4, h), s_z.at[h], r_z.at[h], fwd)

    def dy_copy(h):
        return remote(kv_head(2, h), kv_head(3, h), s_dy.at[h], r_dy.at[h], mate)

    def dz_copy(h):
        return remote(kv_head(4, h), kv_head(5, h), s_dz.at[h], r_dz.at[h], mate)

    dk = remote(kv.at[:, :, pl.ds(0, tok)], kv.at[:, :, pl.ds(tok, tok)], s_dk, r_dk, mate)

    def own_there(h, _):
        for load in own_head(h):
            load.wait()
        return 0

    for h in range(2):
        own_there(h, 0)
        y_copy(h).start()
    spread_across(me).start()
    daud_copy(me).start()
    lax.fori_loop(2, heads, own_there, 0)
    for h in range(2, WINDOW):
        y_copy(h).start()
    dk.start()

    loads[3].wait()
    wide = jnp.concatenate([aqown[...].astype(jnp.float32), jnp.zeros((aud, heads * HD), jnp.float32)], axis=0)
    qx[...] = wide.astype(jnp.bfloat16)

    def dot_t(a, b):
        return lax.dot_general(a, b, (((1,), (1,)), ((), ())), preferred_element_type=jnp.float32)

    lane = lax.broadcasted_iota(jnp.int32, (4 * aud, HD), 1)

    def far_head(h, _):
        s = dot_t(qr[:, cols(h)], kv[h, 0, pl.ds(0, tok)]) * SCALE
        m = jnp.max(s, axis=1, keepdims=True)
        w = jnp.exp2(s - m).astype(jnp.bfloat16)
        total = jnp.sum(w.astype(jnp.float32), axis=1, keepdims=True)
        o = jnp.dot(w, kv[h, 1, pl.ds(0, tok)], preferred_element_type=jnp.float32) / total
        for slot in range(4):
            rows = slice(slot * aud, (slot + 1) * aud)
            part_o[slot, :, cols(h)] = o[rows].astype(part_o.dtype)
            st = part_s[slot]
            st = jnp.where(lane[rows] == h, m[rows], st)
            st = jnp.where(lane[rows] == h + 64, total[rows], st)
            part_s[slot] = st
        return 0

    def bo_copy(slot, device, there):
        return remote(part_o.at[slot], back_o.at[there], s_bo.at[slot], r_bo.at[there], device)

    def bs_copy(slot, device, there):
        return remote(part_s.at[slot], back_s.at[there], s_bs.at[slot], r_bs.at[there], device)

    def far_part():
        for slot, exists, device, there in far:
            @pl.when(exists)
            def _(slot=slot):
                q_arrival(slot).wait_recv()
        for pair in range(2):
            both = jnp.concatenate(
                [aqin[2 * pair].astype(jnp.float32), aqin[2 * pair + 1].astype(jnp.float32)], axis=0)
            qr[pl.ds(2 * aud * pair, 2 * aud), :] = both.astype(jnp.bfloat16)
        part_s[...] = jnp.zeros(part_s.shape, jnp.float32)
        lax.fori_loop(0, heads, far_head, 0)
        for slot, exists, device, there in far:
            @pl.when(exists)
            def _(slot=slot, device=device, there=there):
                bo_copy(slot, device, there).start()
                bs_copy(slot, device, there).start()

    def lay_audio(i, _):
        for j in range(2):
            pair = jnp.concatenate(
                [audio[2 * i, j].astype(jnp.float32), audio[2 * i + 1, j].astype(jnp.float32)], axis=0)
            pair = pair.astype(jnp.bfloat16)
            for h in range(heads):
                kv[h, j, pl.ds(pl.multiple_of(6 * tok + 2 * aud * i, 2 * aud), 2 * aud), :] = pair[:, h * HD:(h + 1) * HD]
        return 0

    near = radius[0]
    count = tile_count[me]

    def is_listed(tile):
        listed = jnp.int32(0)
        for j in range(lmax):
            listed = jnp.where((tile_list[j, me] == tile) & (j < count), 1, listed)
        return listed > 0

    tiles = [me, mate, across, across_chip * 2 + 1 - core, zchip * 2 + core, zchip * 2 + 1 - core]
    see_v, see_a = [], []
    for tile in tiles:
        inside = (tile >= 0) & (tile < n)
        see_v.append(jnp.where(inside & (jnp.abs(tile - me) <= near), 0.0, NEG).astype(jnp.float32))
        see_a.append(jnp.where(inside & is_listed(tile), 0.0, NEG).astype(jnp.float32))
    far_seen = []
    for slot in range(4):
        tile = (chip + (2 if slot < 2 else -2)) * 2 + slot % 2
        ok = (tile >= 0) & (tile < n) & is_listed(tile)
        far_seen.append(jnp.where(ok, 0.0, NEG).astype(jnp.float32))

    span = 6 * tok
    keys = span + n * aud
    lane8 = lax.broadcasted_iota(jnp.int32, (aud, HD), 1)

    def softmax_part(s, biases):
        blocks = [s[:, i * tok:(i + 1) * tok] * SCALE + biases[i] for i in range(len(biases))]
        if s.shape[1] > len(biases) * tok:
            blocks.append(s[:, len(biases) * tok:] * SCALE)
        m = functools.reduce(jnp.maximum, [jnp.max(b, axis=1, keepdims=True) for b in blocks]) if blocks[-1].shape[1] != tok else jnp.max(functools.reduce(jnp.maximum, blocks), axis=1, keepdims=True)
        w = jnp.concatenate([jnp.exp2(b - m).astype(jnp.bfloat16) for b in blocks], axis=1)
        return m, w

    def head(h):
        q = jnp.concatenate([qown[:, cols(h)], qx[:, cols(h)]], axis=0)
        s = dot_t(q, kv[h, 0])
        _, wv = softmax_part(s[:tok], see_v)
        ma, wa = softmax_part(s[tok:, :span], see_a)
        wa = jnp.concatenate([wa, jnp.zeros((2 * aud, keys - span), jnp.bfloat16)], axis=1)
        w = jnp.concatenate([wv, wa], axis=0)
        v = kv[h, 1]
        o = jnp.dot(w, jnp.concatenate([v, jnp.ones((keys, HD), jnp.bfloat16)], axis=1), preferred_element_type=jnp.float32)
        attn[:, cols(h)] = o[:tok, :HD] / o[:tok, HD:]
        oa = o[tok:tok + aud, :HD]
        la = o[tok:tok + aud, HD:]
        ma = ma[:aud]
        peaks, sums = [], []
        for slot in range(4):
            st = back_s[slot]
            peaks.append(jnp.max(jnp.where(lane8 == h, st, NEG), axis=1, keepdims=True) + far_seen[slot])
            sums.append(jnp.sum(jnp.where(lane8 == h + 64, st, 0.0), axis=1, keepdims=True))
        peak = functools.reduce(jnp.maximum, peaks, ma)
        shrink = jnp.exp2(ma - peak)
        oa = oa * shrink
        la = la * shrink
        for slot in range(4):
            share = jnp.exp2(peaks[slot] - peak) * sums[slot]
            oa = oa + back_o[slot, :, cols(h)].astype(jnp.float32) * share
            la = la + share
        aattn[:, cols(h)] = oa / la

    def relay(i, _):
        @pl.when(i < heads)
        def _():
            y_copy(i).wait_recv()

            @pl.when(has_fwd)
            def _():
                z_copy(i).start()

            @pl.when(i + WINDOW < heads)
            def _():
                y_copy(i + WINDOW).start()
            dy_copy(i).start()

        @pl.when((i >= LAG_Z) & (i < heads + LAG_Z) & has_src)
        def _():
            z_copy(i - LAG_Z).wait_recv()
            dz_copy(i - LAG_Z).start()

        @pl.when(i == 0)
        def _():
            column_step(1)

        @pl.when(i == 1)
        def _():
            far_part()
            if rows_all > 2:
                column_step(2)

        @pl.when(i == 2)
        def _():
            def more(d, _):
                column_step(d)
                return 0

            lax.fori_loop(3, rows_all, more, 0)

        @pl.when(i == AUDIO_PASS)
        def _():
            lax.fori_loop(0, rows_all, pass_audio, 0)

        @pl.when(i == AUDIO_READY)
        def _():
            lax.fori_loop(0, chips, take_audio, 0)
            lax.fori_loop(0, chips, lay_audio, 0)
            for slot, exists, device, there in far:
                @pl.when(exists)
                def _(slot=slot):
                    bo_copy(slot, mate, slot).wait_recv()
                    bs_copy(slot, mate, slot).wait_recv()
            dk.wait_recv()

        def attend(h, _):
            dy_copy(h).wait_recv()

            @pl.when(has_src)
            def _():
                dz_copy(h).wait_recv()
            head(h)
            return 0

        lax.fori_loop(done(i - 1), done(i), attend, 0)
        return 0

    def done(i):
        return jnp.clip(jnp.minimum(2 * (i - AUDIO_READY + 1), i - LAG_C + 1), 0, heads)

    lax.fori_loop(0, heads + LAG_C, relay, 0)

    def finish(mixed, gain):
        scale = lax.rsqrt(jnp.mean(mixed * mixed, axis=1, keepdims=True) + EPS)
        return (mixed * scale * gain).astype(jnp.bfloat16)

    loads[4].wait()
    loads[5].wait()
    vout[...] = finish(attn[...], vgain[...].reshape(1, heads * HD))
    aout[...] = finish(aattn[...], again[...].reshape(1, heads * HD))

    for slot, exists, device, there in far:
        @pl.when(exists)
        def _(slot=slot, device=device, there=there):
            q_copy(slot, device, there).wait_send()
            bo_copy(slot, device, there).wait_send()
            bs_copy(slot, device, there).wait_send()

    @pl.when(high)
    def _():
        spread_up(me).wait_send()

    @pl.when(low)
    def _():
        spread_down(me).wait_send()
    spread_across(me).wait_send()

    def column_left(d, _):
        def below(block):
            @pl.when(high)
            def _():
                spread_up(block).wait_send()
            spread_across(block).wait_send()

        def above(block):
            @pl.when(low)
            def _():
                spread_down(block).wait_send()
            spread_across(block).wait_send()

        from_below(d, below)
        from_above(d, above)
        return 0

    lax.fori_loop(1, rows_all, column_left, 0)

    def daudio_left(i, _):
        daud_copy(2 * i + core).wait_send()
        return 0

    lax.fori_loop(0, chips, daudio_left, 0)
    dk.wait_send()

    def heads_left(h, _):
        y_copy(h).wait_send()
        dy_copy(h).wait_send()

        @pl.when(has_fwd)
        def _():
            z_copy(h).wait_send()

        @pl.when(has_src)
        def _():
            dz_copy(h).wait_send()
        return 0

    lax.fori_loop(0, heads, heads_left, 0)


def solution(mesh):
    n = mesh.shape["seq"]
    chips = n // 2

    def on_device(vq, vk, vv, aq, ak, av, radius, tile_list, tile_count, vgain, again):
        tok, width = vq.shape
        aud = aq.shape[0]
        heads = width // HD
        keys = 6 * tok + n * aud
        bf, f32 = jnp.bfloat16, jnp.float32
        dma = pltpu.SemaphoreType.DMA
        per_head = dma((heads,))
        smem = pl.BlockSpec(memory_space=pltpu.SMEM)
        hbm = pl.BlockSpec(memory_space=pltpu.HBM)
        vmem = pl.BlockSpec(memory_space=pltpu.VMEM)
        return pl.pallas_call(
            functools.partial(kernel, n, heads, tok, aud, tile_list.shape[1]),
            out_shape=(jax.ShapeDtypeStruct(vq.shape, bf), jax.ShapeDtypeStruct(aq.shape, bf)),
            in_specs=[smem] * 3 + [hbm] * 8,
            out_specs=(vmem, vmem),
            scratch_shapes=[
                pltpu.VMEM((heads, 2, keys, HD), bf),
                pltpu.VMEM((n, 2, aud, width), bf),
                pltpu.VMEM((tok, width), bf),
                pltpu.VMEM((aud, width), bf),
                pltpu.VMEM((4, aud, width), bf),
                pltpu.VMEM((2 * aud, width), bf),
                pltpu.VMEM((4 * aud, width), bf),
                pltpu.VMEM((4, aud, width), bf),
                pltpu.VMEM((4, aud, HD), f32),
                pltpu.VMEM((4, aud, width), bf),
                pltpu.VMEM((4, aud, HD), f32),
                pltpu.VMEM((tok, width), f32),
                pltpu.VMEM((aud, width), f32),
                pltpu.VMEM((width,), f32),
                pltpu.VMEM((width,), f32),
                dma((6,)), dma((heads, 2)), dma, dma,
                *([per_head] * 8),
                *([dma((n,))] * 6),
                *([dma((4,))] * 6),
            ],
            compiler_params=pltpu.CompilerParams(
                collective_id=0, has_side_effects=True),
        )(radius, tile_list.T, tile_count, vq, vk, vv, aq, ak, av, vgain, again)

    rows = P(("clips", "seq"), None)
    return jax.shard_map(
        on_device,
        mesh=mesh,
        in_specs=(rows,) * 6 + (P(("clips", "seq")), P("clips", None), P("clips"), P(), P()),
        out_specs=(rows, rows),
        check_vma=False,
    )
```

profile of v0, /device:TPU:5, one launch (start us, length us, event | category | flops | bytes accessed | tf_op | source)
XLA Modules:
  0.0 41.6 jit_solution(10046973037380102350)
XLA Ops:
  1.3 37.9 %shard_map.122 = (bf16[128,1536]{1,0:T(8,128)(2,1)}, bf16[8,1536]{1,0:T(8,128)(2,1)}) custom-call(s32[1]{0:T(128)S(6)} %copy.15.radius, s32[5,16]{1,0:T(8,128)} %bitcast.1, s32[16]{0:T(128)} %tile_count.1, bf16[128,1536]{1,0:T(8,128)(2,1)} %vq_hbm.1, bf16[128,1536]{1,0:T(8,128)(2,1)} %vk_hbm.1, bf16[128,1536]{1,0:T(8,128)(2,1)} %vv_hbm.1, ...), custom_call_target="tpu_custom_call" | custom-call | tf_op jit(solution)/shard_map/pallas_call | solution.py:507
  39.2 0.0 copy-start
  39.2 1.8 %copy.16 = bf16[128,1536]{1,0:T(8,128)(2,1)} copy(bf16[128,1536]{1,0:T(8,128)(2,1)} %get-tuple-element.4) | data formatting | bytes 786432
  41.0 0.0 copy-done
  41.0 0.6 %copy.17 = bf16[8,1536]{1,0:T(8,128)(2,1)} copy(bf16[8,1536]{1,0:T(8,128)(2,1)S(1)} %copy-done) | data formatting | bytes 49152
Async XLA Ops:
  39.2 1.8 %copy-start = (bf16[8,1536]{1,0:T(8,128)(2,1)S(1)}, bf16[8,1536]{1,0:T(8,128)(2,1)}, u32[]{:S(2)}) copy-start(bf16[8,1536]{1,0:T(8,128)(2,1)} %get-tuple-element.5) | copy-start | bytes 73732
where the time goes:
time: 41.8 us; the launch traced here: 41.6 us
  Pallas kernels  37.9 us (91%)
  local copies, waits for them, and re-layouts  2.38 us (6%)
  between operations  1.3 us (3%)
    pallas_call x1, Pallas kernels, on_device(): pl.pallas_call(functools.partial(kernel, n, heads, tok, aud, tile_list.sh...  37.9 us
    unnamed x4, local copies, waits for them, and re-layouts  2.38 us

commit v1 on v0

v1 whole, which is shorter than its diff:
```python
import contextlib
import functools

import jax
import jax.numpy as jnp
from jax import lax
from jax.experimental import pallas as pl
from jax.experimental.pallas import tpu as pltpu
from jax.sharding import PartitionSpec as P

HD = 128
RMAX = 2
SPAN = 4
LOG2E = 1.4426950408889634
SCALE = HD ** (-0.5) * LOG2E
NEG = -1e30
EPS = 1e-6
MESH = pl.DeviceIdType.MESH
LAG_Z = 4
LAG_C = 6
FAR_STEPS = 4
COLUMN_1 = 1
COLUMN_2 = 4
COLUMN_3 = 8
CATCH_UP = 5
PAIR = 2
OWN_FIRST = 2


def part(name):
    return contextlib.nullcontext()


def kernel(
    n, heads, tok, aud, lmax,
    radius_hbm, tile_list_hbm, tile_count_hbm,
    vq_hbm, vk_hbm, vv_hbm, aq_hbm, ak_hbm, av_hbm, vgain_hbm, again_hbm,
    attn, aattn, vgain, again,
    radius, tile_list, tile_count,
    kv, audio, qown, aqown, aqin, qx, qr, part_o, part_s, back_o, back_s, tops, sums, atops, asums,
    load_sem, own_sem, s_kv, r_dk, r_y, s_z, r_z, r_d,
    s_col, r_col, s_aud, r_across, r_daud, s_q, r_q, s_bo, r_bo, s_bs, r_bs,
):
    me = lax.axis_index("seq")
    chips = n // 2
    chip = me // 2
    core = me % 2
    mate = chip * 2 + (1 - core)
    odd = chip % 2
    across_chip = chip + 1 - 2 * odd
    across = across_chip * 2 + core
    step = 2 - 4 * odd
    fwd_chip = chip + step
    has_fwd = (fwd_chip >= 0) & (fwd_chip < chips)
    src_chip = chip - step
    has_src = (src_chip >= 0) & (src_chip < chips)
    zchip = chip - 1 + 2 * odd
    fwd = jnp.clip(fwd_chip, 0, chips - 1) * 2 + core

    barrier = pltpu.get_barrier_semaphore()

    def greet(device):
        pl.semaphore_signal(barrier, inc=1, device_id={"seq": device}, device_id_type=MESH)

    low, high = chip >= 2, chip + 2 < chips
    up_to = jnp.clip(chip + 2, 0, chips - 1) * 2 + core
    down_to = jnp.clip(chip - 2, 0, chips - 1) * 2 + core
    greet(across)
    greet(mate)
    for exists, device in ((high, up_to), (low, down_to)):
        @pl.when(exists)
        def _(device=device):
            greet(device)

    loads = [
        pltpu.make_async_copy(aq_hbm, aqown, load_sem.at[0]),
        pltpu.make_async_copy(ak_hbm, audio.at[me, 0], load_sem.at[1]),
        pltpu.make_async_copy(av_hbm, audio.at[me, 1], load_sem.at[1]),
        pltpu.make_async_copy(vq_hbm, qown, load_sem.at[2]),
        pltpu.make_async_copy(vgain_hbm, vgain, load_sem.at[3]),
        pltpu.make_async_copy(again_hbm, again, load_sem.at[4]),
        pltpu.make_async_copy(radius_hbm, radius, load_sem.at[5]),
        pltpu.make_async_copy(tile_list_hbm, tile_list, load_sem.at[6]),
        pltpu.make_async_copy(tile_count_hbm, tile_count, load_sem.at[7]),
    ]

    def cols(h):
        return pl.ds(pl.multiple_of(h * HD, HD), HD)

    def own_head(h):
        return [
            pltpu.make_async_copy(side.at[:, cols(h)], kv.at[h, j, pl.ds(0, tok)], own_sem.at[jnp.minimum(h, OWN_FIRST)])
            for j, side in enumerate((vk_hbm, vv_hbm))
        ]

    for load in loads[:3]:
        load.start()

    def load_own(h, _):
        for load in own_head(h):
            load.start()
        return 0

    lax.fori_loop(0, heads, load_own, 0)
    for load in loads[3:]:
        load.start()

    @pl.when(jnp.logical_not(has_src))
    def _():
        def clear(h, _):
            kv[h, :, pl.ds(3 * tok, tok), :] = jnp.zeros((2, tok, HD), kv.dtype)
            return 0

        lax.fori_loop(0, heads, clear, 0)

    far = [(0, high, up_to), (1, low, down_to)]
    for slot, exists, device in far:
        @pl.when(jnp.logical_not(exists))
        def _(slot=slot):
            aqin[slot] = jnp.zeros(aqin.shape[1:], aqin.dtype)
            back_o[slot] = jnp.zeros(back_o.shape[1:], back_o.dtype)
            back_s[slot] = jnp.zeros(back_s.shape[1:], back_s.dtype)

    with part("barrier"):
        pl.semaphore_wait(barrier, 2 + high.astype(jnp.int32) + low.astype(jnp.int32))

    def remote(src, dst, s, r, device):
        return pltpu.make_async_remote_copy(
            src_ref=src, dst_ref=dst, send_sem=s, recv_sem=r,
            device_id={"seq": device}, device_id_type=MESH)

    def q_copy(slot, device):
        return remote(aqown, aqin.at[1 - slot], s_q.at[slot], r_q.at[1 - slot], device)

    def q_arrival(slot):
        return remote(aqown, aqin.at[slot], s_q.at[slot], r_q.at[slot], mate)

    row, rows_all = chip // 2, chips // 2

    def aud_copy(sem, landed, block, device):
        return remote(audio.at[block], audio.at[block], sem, landed, device)

    def daud_copy(block):
        return aud_copy(s_aud, r_daud, block, mate)

    def spread_up(block):
        return aud_copy(s_col, r_col.at[block // 4], block, up_to)

    def spread_down(block):
        return aud_copy(s_col, r_col.at[block // 4], block, down_to)

    def spread_across(block):
        return aud_copy(s_aud, r_across, block, across)

    def from_below(d, act):
        @pl.when(row - d >= 0)
        def _():
            block = jnp.maximum(me - 4 * d, 0)
            act(block)

    def from_above(d, act):
        @pl.when(row + d < rows_all)
        def _():
            block = jnp.minimum(me + 4 * d, n - 1)
            act(block)

    def column_step(d):
        def below(block):
            spread_up(block).wait_recv()

            @pl.when(high)
            def _():
                spread_up(block).start()
            spread_across(block).start()
            daud_copy(block).start()

        def above(block):
            spread_down(block).wait_recv()

            @pl.when(low)
            def _():
                spread_down(block).start()
            spread_across(block).start()
            daud_copy(block).start()

        from_below(d, below)
        from_above(d, above)

    def several(count, sem):
        blocks = audio.at[pl.ds(0, count)]
        return remote(blocks, blocks, sem, sem, mate)

    def pass_audio():
        several(rows_all, r_across).wait_recv()

        def forward(i, _):
            daud_copy(4 * i + across % 4).start()
            return 0

        lax.fori_loop(0, rows_all, forward, 0)

    def take_audio():
        several(chips, r_daud).wait_recv()

    def kv_head(slot, h):
        return kv.at[h, :, pl.ds(slot * tok, tok)]

    def y_copy(h):
        return remote(kv_head(0, h), kv_head(2, h), s_kv, r_y.at[h], across)

    def z_copy(h):
        return remote(kv_head(2, h), kv_head(3, h), s_z, r_z.at[h], fwd)

    def d_copy(h):
        return remote(kv.at[h, :, pl.ds(2 * tok, 2 * tok)], kv.at[h, :, pl.ds(4 * tok, 2 * tok)], s_kv, r_d.at[h], mate)

    dk = remote(kv.at[:, :, pl.ds(0, tok)], kv.at[:, :, pl.ds(tok, tok)], s_kv, r_dk, mate)

    def own_there(first, count):
        there = kv.at[pl.ds(first, count), :, pl.ds(0, tok)]
        pltpu.make_async_copy(there, there, own_sem.at[min(first, OWN_FIRST)]).wait()

    for h in range(OWN_FIRST):
        own_there(h, 1)
        y_copy(h).start()
    loads[0].wait()
    for slot, exists, device in far:
        @pl.when(exists)
        def _(slot=slot, device=device):
            q_copy(slot, device).start()
    pltpu.make_async_copy(audio.at[me], audio.at[me], load_sem.at[1]).wait()

    @pl.when(high)
    def _():
        spread_up(me).start()

    @pl.when(low)
    def _():
        spread_down(me).start()
    own_there(OWN_FIRST, heads - OWN_FIRST)
    for h in range(OWN_FIRST, heads):
        y_copy(h).start()
    spread_across(me).start()
    daud_copy(me).start()
    dk.start()

    for load in loads[3:9]:
        load.wait()
    wide = jnp.concatenate([aqown[...].astype(jnp.float32), jnp.zeros((aud, heads * HD), jnp.float32)], axis=0)
    qx[...] = wide.astype(jnp.bfloat16)

    def dot_t(a, b):
        return lax.dot_general(a, b, (((1,), (1,)), ((), ())), preferred_element_type=jnp.float32)

    def is_listed(block, tile):
        listed = jnp.int32(0)
        for j in range(lmax):
            listed = jnp.where((tile_list[j, block] == tile) & (j < tile_count[block]), 1, listed)
        return listed > 0

    def bias_of(seen):
        return jnp.where(seen, 0.0, NEG).astype(jnp.float32)

    tiles = [me, mate, across, zchip * 2 + core, across_chip * 2 + 1 - core, zchip * 2 + 1 - core]
    near = radius[0]
    see_v, see_a = [], []
    for tile in tiles:
        inside = (tile >= 0) & (tile < n)
        see_v.append(bias_of(inside & (jnp.abs(tile - me) <= near)))
        see_a.append(bias_of(inside & is_listed(me, tile)))
    upper = lax.broadcasted_iota(jnp.int32, (2 * aud, tok), 0) < aud
    see_far = [
        jnp.where(upper, bias_of(is_listed(up_to, tile)), bias_of(is_listed(down_to, tile)))
        for tile in (me, mate)
    ]
    far_there = [bias_of(exists) for _, exists, _ in far]

    lane = lax.broadcasted_iota(jnp.int32, (aud, HD), 1)

    def far_group(hs):
        loaded = [(qr[:, cols(h)], kv[h, 0, pl.ds(0, 2 * tok)], kv[h, 1, pl.ds(0, 2 * tok)]) for h in hs]
        scores = [dot_t(q, k) for q, k, _ in loaded]
        results = []
        for s, (_, _, v) in zip(scores, loaded):
            sides = [s[:, j * tok:(j + 1) * tok] * SCALE + see_far[j] for j in range(2)]
            m = jnp.max(jnp.maximum(*sides), axis=1, keepdims=True)
            w = jnp.concatenate([jnp.exp2(side - m).astype(jnp.bfloat16) for side in sides], axis=1)
            ones = jnp.ones((2 * tok, HD), jnp.bfloat16)
            results.append((m, jnp.dot(w, jnp.concatenate([v, ones], axis=1), preferred_element_type=jnp.float32)))
        stats = [part_s[slot] for slot in range(2)]
        for h, (m, o) in zip(hs, results):
            mean = (o[:, :HD] / o[:, HD:]).astype(part_o.dtype).astype(jnp.float32)
            for slot in range(2):
                rows = slice(slot * aud, (slot + 1) * aud)
                part_o[slot, :, cols(h)] = mean[rows].astype(part_o.dtype)
                stats[slot] = jnp.where(lane == h, m[rows], stats[slot])
                stats[slot] = jnp.where(lane == h + 64, o[rows, HD:], stats[slot])
        for slot in range(2):
            part_s[slot] = stats[slot]

    def bo_copy(slot, device):
        return remote(part_o.at[slot], back_o.at[1 - slot], s_bo.at[slot], r_bo.at[1 - slot], device)

    def bs_copy(slot, device):
        return remote(part_s.at[slot], back_s.at[1 - slot], s_bs.at[slot], r_bs.at[1 - slot], device)

    def far_open():
        dk.wait_recv()
        for slot, exists, device in far:
            @pl.when(exists)
            def _(slot=slot):
                q_arrival(slot).wait_recv()
        both = jnp.concatenate([aqin[0].astype(jnp.float32), aqin[1].astype(jnp.float32)], axis=0)
        qr[...] = both.astype(jnp.bfloat16)
        part_s[...] = jnp.zeros(part_s.shape, jnp.float32)

    far_each = -(-heads // FAR_STEPS)

    def far_some(i):
        far_group([jnp.minimum(i * far_each + j, heads - 1) for j in range(far_each)])

    def far_close():
        for slot, exists, device in far:
            @pl.when(exists)
            def _(slot=slot, device=device):
                bo_copy(slot, device).start()
                bs_copy(slot, device).start()

    def lay_audio(i, _):
        for j in range(2):
            pair = jnp.concatenate(
                [audio[2 * i, j].astype(jnp.float32), audio[2 * i + 1, j].astype(jnp.float32)], axis=0)
            pair = pair.astype(jnp.bfloat16)
            for h in range(heads):
                kv[h, j, pl.ds(pl.multiple_of(6 * tok + 2 * aud * i, 2 * aud), 2 * aud), :] = pair[:, h * HD:(h + 1) * HD]
        return 0

    span = 6 * tok
    keys = span + n * aud

    def softmax_part(s, biases):
        blocks = [s[:, i * tok:(i + 1) * tok] * SCALE + biases[i] for i in range(len(biases))]
        if s.shape[1] > len(biases) * tok:
            blocks.append(s[:, len(biases) * tok:] * SCALE)
        m = functools.reduce(jnp.maximum, [jnp.max(b, axis=1, keepdims=True) for b in blocks]) if blocks[-1].shape[1] != tok else jnp.max(functools.reduce(jnp.maximum, blocks), axis=1, keepdims=True)
        w = jnp.concatenate([jnp.exp2(b - m).astype(jnp.bfloat16) for b in blocks], axis=1)
        return m, w

    def merge(h, oa, la, ma, stats, far_o):
        peaks, totals = [], []
        for slot in range(2):
            st = stats[slot]
            peaks.append(jnp.max(jnp.where(lane == h, st, NEG), axis=1, keepdims=True) + far_there[slot])
            totals.append(jnp.sum(jnp.where(lane == h + 64, st, 0.0), axis=1, keepdims=True))
        peak = functools.reduce(jnp.maximum, peaks, ma)
        shrink = jnp.exp2(ma - peak)
        oa = oa * shrink
        la = la * shrink
        for slot in range(2):
            share = jnp.exp2(peaks[slot] - peak) * totals[slot]
            oa = oa + far_o[slot].astype(jnp.float32) * share
            la = la + share
        return oa / la

    def far_back(hs):
        return [back_s[slot] for slot in range(2)], [[back_o[slot, :, cols(h)] for slot in range(2)] for h in hs]

    def mix(hs, width):
        qs = [jnp.concatenate([qown[:, cols(h)], qx[:, cols(h)]], axis=0) for h in hs]
        ks = [kv[h, 0, pl.ds(0, width)] for h in hs]
        vs = [jnp.concatenate([kv[h, 1, pl.ds(0, width)], jnp.ones((width, HD), jnp.bfloat16)], axis=1) for h in hs]
        scores = [dot_t(q, k) for q, k in zip(qs, ks)]
        weights = []
        for s in scores:
            mv, wv = softmax_part(s[:tok], see_v)
            ma, wa = softmax_part(s[tok:, :span], see_a)
            if width > span:
                wa = jnp.concatenate([wa, jnp.zeros((2 * aud, width - span), jnp.bfloat16)], axis=1)
            weights.append((mv, ma[:aud], jnp.concatenate([wv, wa], axis=0)))
        return [(mv, ma, jnp.dot(w, v, preferred_element_type=jnp.float32)) for (mv, ma, w), v in zip(weights, vs)]

    def heads_full(hs):
        stats, far_o = far_back(hs)
        mixed = mix(hs, keys)
        merged = [merge(h, o[tok:tok + aud, :HD], o[tok:tok + aud, HD:], ma, stats, f)
                  for h, (_, ma, o), f in zip(hs, mixed, far_o)]
        for h, (_, _, o), joined in zip(hs, mixed, merged):
            attn[:, cols(h)] = o[:tok, :HD] / o[:tok, HD:]
            aattn[:, cols(h)] = joined

    def heads_video(hs):
        for h, (mv, ma, o) in zip(hs, mix(hs, span)):
            attn[:, cols(h)] = o[:tok, :HD]
            sums[h] = o[:tok, HD:]
            tops[h] = jnp.broadcast_to(mv, (tok, HD))
            aattn[:, cols(h)] = o[tok:tok + aud, :HD]
            asums[h] = o[tok:tok + aud, HD:]
            atops[h] = jnp.broadcast_to(ma, (aud, HD))

    def heads_audio(hs):
        stats, far_o = far_back(hs)
        loaded = [
            (qown[:, cols(h)], kv[h, 0, pl.ds(span, n * aud)],
             jnp.concatenate([kv[h, 1, pl.ds(span, n * aud)], jnp.ones((n * aud, HD), jnp.bfloat16)], axis=1))
            for h in hs]
        held = [(attn[:, cols(h)], sums[h], tops[h], aattn[:, cols(h)], asums[h], atops[h]) for h in hs]
        scores = [dot_t(q, k) * SCALE for q, k, _ in loaded]
        peaks = [jnp.maximum(jnp.max(s, axis=1, keepdims=True), top) for s, (_, _, top, _, _, _) in zip(scores, held)]
        mixed = [
            jnp.dot(jnp.exp2(s - peak[:, :1]).astype(jnp.bfloat16), v, preferred_element_type=jnp.float32)
            for s, peak, (_, _, v) in zip(scores, peaks, loaded)]
        merged = [merge(h, oa, la, ma, stats, f) for h, (_, _, _, oa, la, ma), f in zip(hs, held, far_o)]
        for h, o, peak, (old, total, top, _, _, _), joined in zip(hs, mixed, peaks, held, merged):
            shrink = jnp.exp2(top - peak)
            attn[:, cols(h)] = (old * shrink + o[:, :HD]) / (total * shrink + o[:, HD:])
            aattn[:, cols(h)] = joined

    def sent():
        for slot, exists, device in far:
            @pl.when(exists)
            def _(slot=slot, device=device):
                q_copy(slot, device).wait_send()
                bo_copy(slot, device).wait_send()
                bs_copy(slot, device).wait_send()

        @pl.when(high & low)
        def _():
            several(rows_all + 1, s_col).wait_send()

        @pl.when(high != low)
        def _():
            several(1, s_col).wait_send()
        several(3 * rows_all, s_aud).wait_send()

    audio_ready = heads + LAG_Z - 1
    early = heads // PAIR - 1

    def relay(i, _):
        @pl.when(i < heads)
        def _():
            with part("ywait"):
                y_copy(i).wait_recv()

            @pl.when(has_fwd)
            def _():
                z_copy(i).start()


        @pl.when((i >= LAG_Z) & (i < heads + LAG_Z))
        def _():
            @pl.when(has_src)
            def _():
                with part("zwait"):
                    z_copy(i - LAG_Z).wait_recv()
            d_copy(i - LAG_Z).start()

        @pl.when(i == COLUMN_1)
        def _():
            with part("col1"):
                column_step(1)

        @pl.when(i == 0)
        def _():
            with part("faropen"):
                far_open()

        @pl.when(i == COLUMN_2)
        def _():
            if rows_all > 2:
                with part("col2"):
                    column_step(2)

        @pl.when(i == COLUMN_3)
        def _():
            def more(d, _):
                column_step(d)
                return 0

            with part("col3"):
                lax.fori_loop(3, rows_all, more, 0)

        @pl.when(i < FAR_STEPS)
        def _():
            with part("far"):
                far_some(i)

        @pl.when(i == FAR_STEPS - 1)
        def _():
            far_close()

        @pl.when(i == audio_ready - 1)
        def _():
            with part("passaudio"):
                pass_audio()

        @pl.when(i == audio_ready)
        def _():
            with part("takeaudio"):
                take_audio()
            with part("layaudio"):
                lax.fori_loop(0, chips, lay_audio, 0)
            with part("bowait"):
                for slot, exists, device in far:
                    @pl.when(exists)
                    def _(slot=slot):
                        bo_copy(1 - slot, mate).wait_recv()
                        bs_copy(1 - slot, mate).wait_recv()
            with part("sent"):
                sent()

        def arrive(hs):
            with part("dwait"):
                for h in hs:
                    d_copy(h).wait_recv()

        def attend_video(p, _):
            hs = [p * PAIR + k for k in range(PAIR)]
            arrive(hs)
            with part("vhead"):
                heads_video(hs)
            return 0

        def attend_audio(g, _):
            with part("ahead"):
                heads_audio([g * CATCH_UP + k for k in range(CATCH_UP)])
            return 0

        def attend(p, _):
            hs = [p * PAIR + k for k in range(PAIR)]
            arrive(hs)
            with part("head"):
                heads_full(hs)
            return 0

        lax.fori_loop(jnp.minimum(pairs(i - 1), early), jnp.minimum(pairs(i), early), attend_video, 0)
        lax.fori_loop(caught(i - 1), caught(i), attend_audio, 0)
        lax.fori_loop(jnp.maximum(pairs(i - 1), early), jnp.maximum(pairs(i), early), attend, 0)
        return 0

    def pairs(i):
        due = jnp.where(i < heads, i - LAG_C + 1, jnp.where(i <= audio_ready, i - LAG_Z, heads))
        return jnp.clip(due // PAIR, 0, heads // PAIR)

    def caught(i):
        return jnp.clip(early * PAIR * (i - audio_ready + 1) // CATCH_UP, 0, early * PAIR // CATCH_UP)

    lax.fori_loop(0, heads + LAG_Z + 1, relay, 0)

    with part("drain"):
        kv_sent = kv.at[:, :, pl.ds(0, 4 * tok)]
        remote(kv_sent, kv_sent, s_kv, r_dk, mate).wait_send()

        @pl.when(has_fwd)
        def _():
            z_sent = kv.at[:, :, pl.ds(0, tok)]
            remote(z_sent, z_sent, s_z, r_dk, mate).wait_send()


def finish_kernel(attn, aattn, vgain, again, vout, aout):
    def finish(mixed, gain):
        scale = lax.rsqrt(jnp.mean(mixed * mixed, axis=1, keepdims=True) + EPS)
        return (mixed * scale * gain[...].reshape(1, mixed.shape[1])).astype(jnp.bfloat16)

    vout[...] = finish(attn[...], vgain)
    aout[...] = finish(aattn[...], again)


def solution(mesh):
    n = mesh.shape["seq"]
    chips = n // 2

    def on_device(vq, vk, vv, aq, ak, av, radius, tile_list, tile_count, vgain, again):
        tok, width = vq.shape
        aud = aq.shape[0]
        heads = width // HD
        keys = 6 * tok + n * aud
        bf, f32 = jnp.bfloat16, jnp.float32
        dma = pltpu.SemaphoreType.DMA
        per_head = dma((heads,))
        hbm = pl.BlockSpec(memory_space=pltpu.HBM)
        vmem = pl.BlockSpec(memory_space=pltpu.VMEM)
        mixed = pl.pallas_call(
            functools.partial(kernel, n, heads, tok, aud, tile_list.shape[1]),
            out_shape=(
                pltpu.VMEM((tok, width), f32), pltpu.VMEM((aud, width), f32),
                pltpu.VMEM((width,), f32), pltpu.VMEM((width,), f32),
            ),
            in_specs=[hbm] * 11,
            out_specs=(vmem,) * 4,
            scratch_shapes=[
                pltpu.SMEM(radius.shape, jnp.int32),
                pltpu.SMEM(tile_list.shape[::-1], jnp.int32),
                pltpu.SMEM(tile_count.shape, jnp.int32),
                pltpu.VMEM((heads, 2, keys, HD), bf),
                pltpu.VMEM((n, 2, aud, width), bf),
                pltpu.VMEM((tok, width), bf),
                pltpu.VMEM((aud, width), bf),
                pltpu.VMEM((2, aud, width), bf),
                pltpu.VMEM((2 * aud, width), bf),
                pltpu.VMEM((2 * aud, width), bf),
                pltpu.VMEM((2, aud, width), bf),
                pltpu.VMEM((2, aud, HD), f32),
                pltpu.VMEM((2, aud, width), bf),
                pltpu.VMEM((2, aud, HD), f32),
                *([pltpu.VMEM((heads, tok, HD), f32)] * 2),
                *([pltpu.VMEM((heads, aud, HD), f32)] * 2),
                dma((8,)), dma((OWN_FIRST + 1,)), dma, dma,
                per_head, dma, per_head, per_head,
                dma, dma((chips // 2,)), dma, dma, dma,
                *([dma((2,))] * 6),
            ],
            compiler_params=pltpu.CompilerParams(
                collective_id=0, has_side_effects=True),
        )(radius, tile_list.T, tile_count, vq, vk, vv, aq, ak, av, vgain, again)
        return pl.pallas_call(
            finish_kernel,
            out_shape=(jax.ShapeDtypeStruct(vq.shape, bf), jax.ShapeDtypeStruct(aq.shape, bf)),
            in_specs=[vmem] * 4,
            out_specs=(vmem, vmem),
            compiler_params=pltpu.CompilerParams(vmem_limit_bytes=8 * 1024 * 1024),
        )(*mixed)

    rows = P(("clips", "seq"), None)
    return jax.shard_map(
        on_device,
        mesh=mesh,
        in_specs=(rows,) * 6 + (P(("clips", "seq")), P("clips", None), P("clips"), P(), P()),
        out_specs=(rows, rows),
        check_vma=False,
    )
```

time: 41.8 us -> 32.4 us (0.78)
  Pallas kernels: 37.9 us -> 30.8 us
  local copies, waits for them, and re-layouts: 2.38 us -> 0 us
    pallas_call x1, Pallas kernels: 37.9 us -> 29.9 us  [on_device(): pl.pallas_call(functools.partial(kernel, n, heads, tok, aud, tile_list.sh...]
    unnamed x4 -> x0, local copies, waits for them, and re-layouts: 2.38 us -> none
    pallas_call x0 -> x1, Pallas kernels: none -> 0.93 us  [on_device(): pl.pallas_call(finish_kernel, out_shape=(jax.ShapeDtypeStruct(vq.shape, b...]
where the time goes in v1:
time: 32.4 us; the launch traced here: 32.1 us
  Pallas kernels  30.8 us (95%)
  between operations  1.29 us (4%)
    pallas_call x1, Pallas kernels, on_device(): pl.pallas_call(functools.partial(kernel, n, heads, tok, aud, tile_list.sh...  29.9 us
    pallas_call x1, Pallas kernels, on_device(): pl.pallas_call(finish_kernel, out_shape=(jax.ShapeDtypeStruct(vq.shape, b...  0.93 us

profile of v1, /device:TPU:5, one launch (start us, length us, event | category | flops | bytes accessed | tf_op | source)
XLA Modules:
  0.0 32.1 jit_solution(13213400385080887900)
XLA Ops:
  1.3 29.9 %shard_map.122 = (f32[128,1536]{1,0:T(8,128)S(1)}, f32[8,1536]{1,0:T(8,128)S(1)}, f32[1536]{0:T(1024)S(1)}, f32[1536]{0:T(1024)S(1)}) custom-call(s32[1]{0:T(128)S(6)} %copy.13.radius_hbm, s32[5,16]{1,0:T(8,128)} %bitcast.1, s32[16]{0:T(128)} %tile_count_hbm.1, bf16[128,1536]{1,0:T(8,128)(2,1)} %vq_hbm.1, bf16[128,1536]{1,0:T(8,128)(2,1)} %vk_hbm.1, ...), custom_call_target="tpu_custom_call" | custom-call | tf_op jit(solution)/shard_map/pallas_call | solution.py:582
  31.2 0.9 %shard_map.123 = (bf16[128,1536]{1,0:T(8,128)(2,1)}, bf16[8,1536]{1,0:T(8,128)(2,1)}) custom-call(f32[128,1536]{1,0:T(8,128)S(1)} %get-tuple-element.6.attn, f32[8,1536]{1,0:T(8,128)S(1)} %get-tuple-element.7.aattn, f32[1536]{0:T(1024)S(1)} %get-tuple-element.8.vgain, f32[1536]{0:T(1024)S(1)} %get-tuple-element.9.again), custom_call_target="tpu_custom_call" | custom-call | tf_op jit(solution)/shard_map/pallas_call | solution.py:615

commit v2 on v1

--- a/solution.py
+++ b/solution.py
@@ -17,11 +17,13 @@
 EPS = 1e-6
 MESH = pl.DeviceIdType.MESH
 LAG_Z = 4
-LAG_C = 6
 FAR_STEPS = 4
-COLUMN_1 = 1
-COLUMN_2 = 4
-COLUMN_3 = 8
+WAVES = (1, 4, 6, 8)
+BESIDE = 9
+WINDOW = 4
+FIRST_PIECES = 2
+LAST_PIECES = 4
+MAIN_PAIRS = 3
 CATCH_UP = 5
 PAIR = 2
 OWN_FIRST = 2
@@ -39,7 +41,7 @@
     radius, tile_list, tile_count,
     kv, audio, qown, aqown, aqin, qx, qr, part_o, part_s, back_o, back_s, tops, sums, atops, asums,
     load_sem, own_sem, s_kv, r_dk, r_y, s_z, r_z, r_d,
-    s_col, r_col, s_aud, r_across, r_daud, s_q, r_q, s_bo, r_bo, s_bs, r_bs,
+    s_link, r_aud, s_aud, r_daud, s_q, r_q, s_bo, r_bo, s_bs, r_bs,
 ):
     me = lax.axis_index("seq")
     chips = n // 2
@@ -143,61 +145,83 @@
     def daud_copy(block):
         return aud_copy(s_aud, r_daud, block, mate)
 
-    def spread_up(block):
-        return aud_copy(s_col, r_col.at[block // 4], block, up_to)
-
-    def spread_down(block):
-        return aud_copy(s_col, r_col.at[block // 4], block, down_to)
-
-    def spread_across(block):
-        return aud_copy(s_aud, r_across, block, across)
-
-    def from_below(d, act):
-        @pl.when(row - d >= 0)
-        def _():
-            block = jnp.maximum(me - 4 * d, 0)
-            act(block)
-
-    def from_above(d, act):
-        @pl.when(row + d < rows_all)
-        def _():
-            block = jnp.minimum(me + 4 * d, n - 1)
-            act(block)
-
-    def column_step(d):
-        def below(block):
-            spread_up(block).wait_recv()
-
-            @pl.when(high)
+    def link_copy(block, device):
+        return aud_copy(s_link, r_aud.at[block // 2], block, device)
+
+    turn = 1 - 2 * odd
+    ahead = jnp.where(odd == 1, row, rows_all - 1 - row)
+    behind = rows_all - 1 - ahead
+    back = jnp.clip(src_chip, 0, chips - 1) * 2 + core
+
+    def at_level(block, k):
+        return jnp.clip(block + 4 * k * turn, 0, n - 1)
+
+    def send_on(block):
+        @pl.when(has_src)
+        def _():
+            link_copy(block, back).start()
+
+    def to_front(block):
+        @pl.when(has_fwd)
+        def _():
+            link_copy(block, fwd).start()
+
+    def wave(first, k):
+        @pl.when(k <= ahead)
+        def _():
+            block = at_level(first, k)
+            link_copy(block, back).wait_recv()
+            send_on(block)
+            daud_copy(block).start()
+
+            @pl.when(jnp.logical_not(has_src))
             def _():
-                spread_up(block).start()
-            spread_across(block).start()
-            daud_copy(block).start()
-
-        def above(block):
-            spread_down(block).wait_recv()
-
-            @pl.when(low)
-            def _():
-                spread_down(block).start()
-            spread_across(block).start()
-            daud_copy(block).start()
-
-        from_below(d, below)
-        from_above(d, above)
+                to_across(first, k)
+
+    def to_across(first, k):
+        @pl.when((k >= 2) & (k <= ahead))
+        def _():
+            link_copy(at_level(first, k), across).start()
+
+    def wave_step(k):
+        @pl.when(k == 0)
+        def _():
+            link_copy(across, back).wait_recv()
+            send_on(across)
+            to_front(across)
+            daud_copy(across).start()
+
+        @pl.when(k > 0)
+        def _():
+            wave(across, k)
+        wave(me, k + 1)
+
+    def from_behind(k):
+        @pl.when(k <= behind)
+        def _():
+            for first in (me, across):
+                block = at_level(first, -k)
+                link_copy(block, across).wait_recv()
+                daud_copy(block).start()
 
     def several(count, sem):
         blocks = audio.at[pl.ds(0, count)]
         return remote(blocks, blocks, sem, sem, mate)
 
     def pass_audio():
-        several(rows_all, r_across).wait_recv()
-
-        def forward(i, _):
-            daud_copy(4 * i + across % 4).start()
+        def forward(k, _):
+            from_behind(k)
             return 0
 
-        lax.fori_loop(0, rows_all, forward, 0)
+        lax.fori_loop(2, rows_all, forward, 0)
+
+    def late_across():
+        def send(k, _):
+            to_across(me, k)
+            to_across(across, k)
+            return 0
+
+        lax.fori_loop(2, rows_all, send, 0)
 
     def take_audio():
         several(chips, r_daud).wait_recv()
@@ -205,14 +229,34 @@
     def kv_head(slot, h):
         return kv.at[h, :, pl.ds(slot * tok, tok)]
 
+    last = heads - 1
+
     def y_copy(h):
-        return remote(kv_head(0, h), kv_head(2, h), s_kv, r_y.at[h], across)
+        return remote(kv_head(0, h), kv_head(2, h), s_kv, r_y.at[FIRST_PIECES + h - 1], across)
 
     def z_copy(h):
-        return remote(kv_head(2, h), kv_head(3, h), s_z, r_z.at[h], fwd)
-
-    def d_copy(h):
-        return remote(kv.at[h, :, pl.ds(2 * tok, 2 * tok)], kv.at[h, :, pl.ds(4 * tok, 2 * tok)], s_kv, r_d.at[h], mate)
+        return remote(kv_head(2, h), kv_head(3, h), s_z, r_z.at[FIRST_PIECES + h - 1], fwd)
+
+    def pieces(h):
+        return FIRST_PIECES if h == 0 else LAST_PIECES
+
+    def piece(slot, h, p):
+        count = tok // pieces(h)
+        return kv.at[h, :, pl.ds(slot * tok + p * count, count)]
+
+    def piece_sem(h, p):
+        return (0 if h == 0 else FIRST_PIECES + heads - 2) + p
+
+    def y_piece(h, p):
+        return remote(piece(0, h, p), piece(2, h, p), s_kv, r_y.at[piece_sem(h, p)], across)
+
+    def z_piece(h, p):
+        return remote(piece(2, h, p), piece(3, h, p), s_z, r_z.at[piece_sem(h, p)], fwd)
+
+    def d_copy(p):
+        heads_of = pl.ds(PAIR * p, PAIR)
+        return remote(
+            kv.at[heads_of, :, pl.ds(2 * tok, 2 * tok)], kv.at[heads_of, :, pl.ds(4 * tok, 2 * tok)], s_kv, r_d.at[p], mate)
 
     dk = remote(kv.at[:, :, pl.ds(0, tok)], kv.at[:, :, pl.ds(tok, tok)], s_kv, r_dk, mate)
 
@@ -220,7 +264,12 @@
         there = kv.at[pl.ds(first, count), :, pl.ds(0, tok)]
         pltpu.make_async_copy(there, there, own_sem.at[min(first, OWN_FIRST)]).wait()
 
-    for h in range(OWN_FIRST):
+    own_there(0, 1)
+    for p in range(FIRST_PIECES):
+        y_piece(0, p).start()
+    pltpu.make_async_copy(audio.at[me], audio.at[me], load_sem.at[1]).wait()
+    link_copy(me, across).start()
+    for h in range(1, OWN_FIRST):
         own_there(h, 1)
         y_copy(h).start()
     loads[0].wait()
@@ -228,19 +277,12 @@
         @pl.when(exists)
         def _(slot=slot, device=device):
             q_copy(slot, device).start()
-    pltpu.make_async_copy(audio.at[me], audio.at[me], load_sem.at[1]).wait()
-
-    @pl.when(high)
-    def _():
-        spread_up(me).start()
-
-    @pl.when(low)
-    def _():
-        spread_down(me).start()
+
+    send_on(me)
+    to_front(me)
     own_there(OWN_FIRST, heads - OWN_FIRST)
-    for h in range(OWN_FIRST, heads):
+    for h in range(OWN_FIRST, WINDOW):
         y_copy(h).start()
-    spread_across(me).start()
     daud_copy(me).start()
     dk.start()
 
@@ -415,7 +457,7 @@
             attn[:, cols(h)] = (old * shrink + o[:, :HD]) / (total * shrink + o[:, HD:])
             aattn[:, cols(h)] = joined
 
-    def sent():
+    def far_sent():
         for slot, exists, device in far:
             @pl.when(exists)
             def _(slot=slot, device=device):
@@ -423,20 +465,87 @@
                 bo_copy(slot, device).wait_send()
                 bs_copy(slot, device).wait_send()
 
-        @pl.when(high & low)
-        def _():
-            several(rows_all + 1, s_col).wait_send()
-
-        @pl.when(high != low)
-        def _():
-            several(1, s_col).wait_send()
-        several(3 * rows_all, s_aud).wait_send()
-
-    audio_ready = heads + LAG_Z - 1
-    early = heads // PAIR - 1
+    def audio_sent():
+        several(chips, s_aud).wait_send()
+        for k in range(rows_all):
+            count = 1 + (2 + 2 * k) * (k < rows_all - 1) + 2 * (k > 0) + 2 * max(0, k - 1)
+
+            @pl.when(ahead == k)
+            def _(count=count):
+                several(count, s_link).wait_send()
+
+    pairs = heads // PAIR
+    edge = has_src & jnp.logical_not(has_fwd)
+    late = has_fwd & (behind >= 2)
+
+    def z_due(i):
+        inner = i - LAG_Z + 1 + (edge & (i >= 9)).astype(jnp.int32)
+        return jnp.clip(jnp.where(has_src, inner, i + 1), 0, heads)
+
+    def v_due(i):
+        inner = jnp.clip((i - LAG_Z) // PAIR, 0, MAIN_PAIRS)
+        return jnp.where(has_src, inner, jnp.clip(jnp.where(i < FAR_STEPS, 0, (i - 1) // PAIR), 0, pairs - 1))
+
+    def last_out():
+        for p in range(LAST_PIECES):
+            y_piece(last, p).start()
+
+    def take_y(h):
+        for p in range(pieces(h)):
+            with part("ywaitp"):
+                y_piece(h, p).wait_recv()
+
+            @pl.when(has_fwd)
+            def _(p=p):
+                z_piece(h, p).start()
+
+    def take_z(k, _):
+        @pl.when(has_src & (k > 0) & (k < last))
+        def _():
+            with part("zwait"):
+                z_copy(k).wait_recv()
+
+        for h in (0, last):
+            @pl.when(has_src & (k == h))
+            def _(h=h):
+                with part("zwaitp"):
+                    for p in range(pieces(h)):
+                        z_piece(h, p).wait_recv()
+
+        @pl.when((k % PAIR == PAIR - 1) & jnp.logical_not(edge & (k == last)))
+        def _():
+            d_copy(k // PAIR).start()
+        return 0
+
+    def arrive(p):
+        with part("dwait"):
+            d_copy(p).wait_recv()
+
+    def attend_video(p, _):
+        arrive(p)
+        with part("vhead"):
+            heads_video([p * PAIR + k for k in range(PAIR)])
+        return 0
+
+    def attend_audio(g, _):
+        with part("ahead"):
+            heads_audio([g * CATCH_UP + k for k in range(CATCH_UP)])
+        return 0
+
+    def audio_in():
+        with part("takeaudio"):
+            take_audio()
+        with part("layaudio"):
+            lax.fori_loop(0, chips, lay_audio, 0)
+        with part("bowait"):
+            for slot, exists, device in far:
+                @pl.when(exists)
+                def _(slot=slot):
+                    bo_copy(1 - slot, mate).wait_recv()
+                    bs_copy(1 - slot, mate).wait_recv()
 
     def relay(i, _):
-        @pl.when(i < heads)
+        @pl.when((i > 0) & (i < last))
         def _():
             with part("ywait"):
                 y_copy(i).wait_recv()
@@ -445,40 +554,29 @@
             def _():
                 z_copy(i).start()
 
-
-        @pl.when((i >= LAG_Z) & (i < heads + LAG_Z))
-        def _():
-            @pl.when(has_src)
-            def _():
-                with part("zwait"):
-                    z_copy(i - LAG_Z).wait_recv()
-            d_copy(i - LAG_Z).start()
-
-        @pl.when(i == COLUMN_1)
-        def _():
-            with part("col1"):
-                column_step(1)
+        @pl.when(i + WINDOW < last)
+        def _():
+            y_copy(i + WINDOW).start()
+
+        @pl.when((i + WINDOW == last) & has_src)
+        def _():
+            last_out()
+
+        @pl.when(i == 0)
+        def _():
+            take_y(0)
+
+        @pl.when((i == last) & jnp.logical_not(edge))
+        def _():
+            take_y(last)
+
+        lax.fori_loop(z_due(i - 1), z_due(i), take_z, 0)
 
         @pl.when(i == 0)
         def _():
             with part("faropen"):
                 far_open()
 
-        @pl.when(i == COLUMN_2)
-        def _():
-            if rows_all > 2:
-                with part("col2"):
-                    column_step(2)
-
-        @pl.when(i == COLUMN_3)
-        def _():
-            def more(d, _):
-                column_step(d)
-                return 0
-
-            with part("col3"):
-                lax.fori_loop(3, rows_all, more, 0)
-
         @pl.when(i < FAR_STEPS)
         def _():
             with part("far"):
@@ -488,65 +586,71 @@
         def _():
             far_close()
 
-        @pl.when(i == audio_ready - 1)
-        def _():
-            with part("passaudio"):
-                pass_audio()
-
-        @pl.when(i == audio_ready)
-        def _():
-            with part("takeaudio"):
-                take_audio()
-            with part("layaudio"):
-                lax.fori_loop(0, chips, lay_audio, 0)
-            with part("bowait"):
-                for slot, exists, device in far:
-                    @pl.when(exists)
-                    def _(slot=slot):
-                        bo_copy(1 - slot, mate).wait_recv()
-                        bs_copy(1 - slot, mate).wait_recv()
-            with part("sent"):
-                sent()
-
-        def arrive(hs):
-            with part("dwait"):
-                for h in hs:
-                    d_copy(h).wait_recv()
-
-        def attend_video(p, _):
-            hs = [p * PAIR + k for k in range(PAIR)]
-            arrive(hs)
-            with part("vhead"):
-                heads_video(hs)
-            return 0
-
-        def attend_audio(g, _):
-            with part("ahead"):
-                heads_audio([g * CATCH_UP + k for k in range(CATCH_UP)])
-            return 0
-
-        def attend(p, _):
-            hs = [p * PAIR + k for k in range(PAIR)]
-            arrive(hs)
-            with part("head"):
-                heads_full(hs)
-            return 0
-
-        lax.fori_loop(jnp.minimum(pairs(i - 1), early), jnp.minimum(pairs(i), early), attend_video, 0)
-        lax.fori_loop(caught(i - 1), caught(i), attend_audio, 0)
-        lax.fori_loop(jnp.maximum(pairs(i - 1), early), jnp.maximum(pairs(i), early), attend, 0)
+        for k, at in enumerate(WAVES[:-1]):
+            @pl.when(i == at)
+            def _(k=k):
+                with part("wave"):
+                    wave_step(k)
+
+        @pl.when(i == WAVES[-1])
+        def _():
+            def more(k, _):
+                wave_step(k)
+                return 0
+
+            with part("wavelast"):
+                lax.fori_loop(len(WAVES) - 1, rows_all, more, 0)
+
+            @pl.when(jnp.logical_not(has_src))
+            def _():
+                last_out()
+
+        @pl.when(i == BESIDE)
+        def _():
+            with part("beside"):
+                from_behind(1)
+                far_sent()
+
+        @pl.when((i == heads - WINDOW) & has_src)
+        def _():
+            late_across()
+
+        lax.fori_loop(v_due(i - 1), v_due(i), attend_video, 0)
         return 0
 
-    def pairs(i):
-        due = jnp.where(i < heads, i - LAG_C + 1, jnp.where(i <= audio_ready, i - LAG_Z, heads))
-        return jnp.clip(due // PAIR, 0, heads // PAIR)
-
-    def caught(i):
-        return jnp.clip(early * PAIR * (i - audio_ready + 1) // CATCH_UP, 0, early * PAIR // CATCH_UP)
-
-    lax.fori_loop(0, heads + LAG_Z + 1, relay, 0)
+    lax.fori_loop(0, heads, relay, 0)
+
+    groups = PAIR * (pairs - 1) // CATCH_UP
+    soon = jnp.logical_not(edge | late)
+    first_groups = jnp.where(soon, jnp.where(has_src, PAIR * MAIN_PAIRS // CATCH_UP, groups), 0)
+
+    @pl.when(soon)
+    def _():
+        audio_in()
+    lax.fori_loop(0, first_groups, attend_audio, 0)
+    lax.fori_loop(z_due(last), heads - 2, take_z, 0)
+    lax.fori_loop(v_due(last), pairs - 2, attend_video, 0)
+    with part("passaudio"):
+        pass_audio()
+    lax.fori_loop(jnp.maximum(z_due(last), heads - 2), last, take_z, 0)
+    lax.fori_loop(jnp.maximum(v_due(last), pairs - 2), pairs - 1, attend_video, 0)
+    lax.fori_loop(jnp.maximum(z_due(last), last), heads, take_z, 0)
+
+    @pl.when(edge)
+    def _():
+        take_y(last)
+        d_copy(pairs - 1).start()
+
+    @pl.when(jnp.logical_not(soon))
+    def _():
+        audio_in()
+    lax.fori_loop(first_groups, groups, attend_audio, 0)
+    arrive(pairs - 1)
+    with part("head"):
+        heads_full([PAIR * (pairs - 1) + k for k in range(PAIR)])
 
     with part("drain"):
+        audio_sent()
         kv_sent = kv.at[:, :, pl.ds(0, 4 * tok)]
         remote(kv_sent, kv_sent, s_kv, r_dk, mate).wait_send()
 
@@ -605,8 +709,8 @@
                 *([pltpu.VMEM((heads, tok, HD), f32)] * 2),
                 *([pltpu.VMEM((heads, aud, HD), f32)] * 2),
                 dma((8,)), dma((OWN_FIRST + 1,)), dma, dma,
-                per_head, dma, per_head, per_head,
-                dma, dma((chips // 2,)), dma, dma, dma,
+                dma((heads - 2 + FIRST_PIECES + LAST_PIECES,)), dma, dma((heads - 2 + FIRST_PIECES + LAST_PIECES,)), dma((heads // PAIR,)),
+                dma, dma((chips,)), dma, dma,
                 *([dma((2,))] * 6),
             ],
             compiler_params=pltpu.CompilerParams(

time: 32.4 us -> 31.5 us (0.972)
  Pallas kernels: 30.8 us -> 30.1 us
    pallas_call x1, Pallas kernels: 29.9 us -> 29.2 us  [on_device(): pl.pallas_call(functools.partial(kernel, n, heads, tok, aud, tile_list.sh...]
where the time goes in v2:
time: 31.5 us; the launch traced here: 31.4 us
  Pallas kernels  30.1 us (96%)
  between operations  1.29 us (4%)
    pallas_call x1, Pallas kernels, on_device(): pl.pallas_call(functools.partial(kernel, n, heads, tok, aud, tile_list.sh...  29.2 us
    pallas_call x1, Pallas kernels, on_device(): pl.pallas_call(finish_kernel, out_shape=(jax.ShapeDtypeStruct(vq.shape, b...  0.93 us

profile of v2, /device:TPU:5, one launch (start us, length us, event | category | flops | bytes accessed | tf_op | source)
XLA Modules:
  0.0 31.4 jit_solution(10147237176104149869)
XLA Ops:
  1.3 29.2 %shard_map.122 = (f32[128,1536]{1,0:T(8,128)S(1)}, f32[8,1536]{1,0:T(8,128)S(1)}, f32[1536]{0:T(1024)S(1)}, f32[1536]{0:T(1024)S(1)}) custom-call(s32[1]{0:T(128)S(6)} %copy.13.radius_hbm, s32[5,16]{1,0:T(8,128)} %bitcast.1, s32[16]{0:T(128)} %tile_count_hbm.1, bf16[128,1536]{1,0:T(8,128)(2,1)} %vq_hbm.1, bf16[128,1536]{1,0:T(8,128)(2,1)} %vk_hbm.1, ...), custom_call_target="tpu_custom_call" | custom-call | tf_op jit(solution)/shard_map/pallas_call | solution.py:686
  30.4 0.9 %shard_map.123 = (bf16[128,1536]{1,0:T(8,128)(2,1)}, bf16[8,1536]{1,0:T(8,128)(2,1)}) custom-call(f32[128,1536]{1,0:T(8,128)S(1)} %get-tuple-element.6.attn, f32[8,1536]{1,0:T(8,128)S(1)} %get-tuple-element.7.aattn, f32[1536]{0:T(1024)S(1)} %get-tuple-element.8.vgain, f32[1536]{0:T(1024)S(1)} %get-tuple-element.9.again), custom_call_target="tpu_custom_call" | custom-call | tf_op jit(solution)/shard_map/pallas_call | solution.py:719

commit v3 on v2

--- a/solution.py
+++ b/solution.py
@@ -18,12 +18,15 @@
 MESH = pl.DeviceIdType.MESH
 LAG_Z = 4
 FAR_STEPS = 4
-WAVES = (1, 4, 6, 8)
+WAVES = (0, 3, 5, 7)
+WAVES_ALONE = (0, 4, 6, 8)
+FAR_FIRST = 1
 BESIDE = 9
 WINDOW = 4
 FIRST_PIECES = 2
 LAST_PIECES = 4
 MAIN_PAIRS = 3
+OUT_PIECES = 4
 CATCH_UP = 5
 PAIR = 2
 OWN_FIRST = 2
@@ -41,7 +44,7 @@
     radius, tile_list, tile_count,
     kv, audio, qown, aqown, aqin, qx, qr, part_o, part_s, back_o, back_s, tops, sums, atops, asums,
     load_sem, own_sem, s_kv, r_dk, r_y, s_z, r_z, r_d,
-    s_link, r_aud, s_aud, r_daud, s_q, r_q, s_bo, r_bo, s_bs, r_bs,
+    s_link, r_aud, s_aud, r_daud, s_fo, r_q, r_bo, s_bs, r_bs,
 ):
     me = lax.axis_index("seq")
     chips = n // 2
@@ -132,10 +135,12 @@
             device_id={"seq": device}, device_id_type=MESH)
 
     def q_copy(slot, device):
-        return remote(aqown, aqin.at[1 - slot], s_q.at[slot], r_q.at[1 - slot], device)
-
-    def q_arrival(slot):
-        return remote(aqown, aqin.at[slot], s_q.at[slot], r_q.at[slot], mate)
+        return remote(aqown, aqin.at[1 - slot], s_fo, r_q, device)
+
+    def far_pairs(buffer, sem, fold=1):
+        return [
+            (exist, remote(buffer.at[pl.ds(0, count * fold)], buffer.at[pl.ds(0, count * fold)], sem, sem, mate))
+            for exist, count in ((high & low, 2), (high != low, 1))]
 
     row, rows_all = chip // 2, chips // 2
 
@@ -146,7 +151,7 @@
         return aud_copy(s_aud, r_daud, block, mate)
 
     def link_copy(block, device):
-        return aud_copy(s_link, r_aud.at[block // 2], block, device)
+        return aud_copy(s_link, r_aud.at[block // 4], block, device)
 
     turn = 1 - 2 * odd
     ahead = jnp.where(odd == 1, row, rows_all - 1 - row)
@@ -166,18 +171,6 @@
         def _():
             link_copy(block, fwd).start()
 
-    def wave(first, k):
-        @pl.when(k <= ahead)
-        def _():
-            block = at_level(first, k)
-            link_copy(block, back).wait_recv()
-            send_on(block)
-            daud_copy(block).start()
-
-            @pl.when(jnp.logical_not(has_src))
-            def _():
-                to_across(first, k)
-
     def to_across(first, k):
         @pl.when((k >= 2) & (k <= ahead))
         def _():
@@ -186,23 +179,28 @@
     def wave_step(k):
         @pl.when(k == 0)
         def _():
-            link_copy(across, back).wait_recv()
+            several(1, r_aud.at[row]).wait_recv()
             send_on(across)
             to_front(across)
             daud_copy(across).start()
 
-        @pl.when(k > 0)
-        def _():
-            wave(across, k)
-        wave(me, k + 1)
+        @pl.when((k > 0) & (k <= ahead))
+        def _():
+            several(2, r_aud.at[at_level(me, k) // 4]).wait_recv()
+            for first in (me, across):
+                send_on(at_level(first, k))
+                daud_copy(at_level(first, k)).start()
+
+                @pl.when(jnp.logical_not(has_src))
+                def _(first=first):
+                    to_across(first, k)
 
     def from_behind(k):
         @pl.when(k <= behind)
         def _():
+            several(2, r_aud.at[at_level(me, -k) // 4]).wait_recv()
             for first in (me, across):
-                block = at_level(first, -k)
-                link_copy(block, across).wait_recv()
-                daud_copy(block).start()
+                daud_copy(at_level(first, -k)).start()
 
     def several(count, sem):
         blocks = audio.at[pl.ds(0, count)]
@@ -235,7 +233,7 @@
         return remote(kv_head(0, h), kv_head(2, h), s_kv, r_y.at[FIRST_PIECES + h - 1], across)
 
     def z_copy(h):
-        return remote(kv_head(2, h), kv_head(3, h), s_z, r_z.at[FIRST_PIECES + h - 1], fwd)
+        return remote(kv_head(2, h), kv_head(3, h), s_z, r_z.at[h // PAIR], fwd)
 
     def pieces(h):
         return FIRST_PIECES if h == 0 else LAST_PIECES
@@ -251,12 +249,19 @@
         return remote(piece(0, h, p), piece(2, h, p), s_kv, r_y.at[piece_sem(h, p)], across)
 
     def z_piece(h, p):
-        return remote(piece(2, h, p), piece(3, h, p), s_z, r_z.at[piece_sem(h, p)], fwd)
+        return remote(piece(2, h, p), piece(3, h, p), s_z, r_z.at[0 if h == 0 else heads // PAIR], fwd)
 
     def d_copy(p):
         heads_of = pl.ds(PAIR * p, PAIR)
         return remote(
             kv.at[heads_of, :, pl.ds(2 * tok, 2 * tok)], kv.at[heads_of, :, pl.ds(4 * tok, 2 * tok)], s_kv, r_d.at[p], mate)
+
+    def d_last(share):
+        if share == 0:
+            there = [kv.at[pl.ds(last - 1, PAIR), :, pl.ds(slot * tok, tok)] for slot in (2, 4)]
+        else:
+            there = [kv.at[last - PAIR + share, :, pl.ds(slot * tok, tok)] for slot in (3, 5)]
+        return remote(*there, s_kv, r_d.at[last // PAIR], mate)
 
     dk = remote(kv.at[:, :, pl.ds(0, tok)], kv.at[:, :, pl.ds(tok, tok)], s_kv, r_dk, mate)
 
@@ -341,17 +346,15 @@
             part_s[slot] = stats[slot]
 
     def bo_copy(slot, device):
-        return remote(part_o.at[slot], back_o.at[1 - slot], s_bo.at[slot], r_bo.at[1 - slot], device)
+        return remote(part_o.at[slot], back_o.at[1 - slot], s_fo, r_bo, device)
 
     def bs_copy(slot, device):
-        return remote(part_s.at[slot], back_s.at[1 - slot], s_bs.at[slot], r_bs.at[1 - slot], device)
+        return remote(part_s.at[slot], back_s.at[1 - slot], s_bs, r_bs, device)
 
     def far_open():
         dk.wait_recv()
-        for slot, exists, device in far:
-            @pl.when(exists)
-            def _(slot=slot):
-                q_arrival(slot).wait_recv()
+        for exist, copy in far_pairs(aqin, r_q):
+            pl.when(exist)(copy.wait_recv)
         both = jnp.concatenate([aqin[0].astype(jnp.float32), aqin[1].astype(jnp.float32)], axis=0)
         qr[...] = both.astype(jnp.bfloat16)
         part_s[...] = jnp.zeros(part_s.shape, jnp.float32)
@@ -380,13 +383,20 @@
     span = 6 * tok
     keys = span + n * aud
 
+    def row_sum(parts):
+        wide = [p.astype(jnp.float32) for p in parts]
+        same = [p for p in wide if p.shape == wide[0].shape]
+        rest = [p for p in wide if p.shape != wide[0].shape]
+        total = jnp.sum(functools.reduce(jnp.add, same), axis=1, keepdims=True)
+        return functools.reduce(jnp.add, [jnp.sum(p, axis=1, keepdims=True) for p in rest], total)
+
     def softmax_part(s, biases):
         blocks = [s[:, i * tok:(i + 1) * tok] * SCALE + biases[i] for i in range(len(biases))]
         if s.shape[1] > len(biases) * tok:
             blocks.append(s[:, len(biases) * tok:] * SCALE)
         m = functools.reduce(jnp.maximum, [jnp.max(b, axis=1, keepdims=True) for b in blocks]) if blocks[-1].shape[1] != tok else jnp.max(functools.reduce(jnp.maximum, blocks), axis=1, keepdims=True)
-        w = jnp.concatenate([jnp.exp2(b - m).astype(jnp.bfloat16) for b in blocks], axis=1)
-        return m, w
+        parts = [jnp.exp2(b - m).astype(jnp.bfloat16) for b in blocks]
+        return m, row_sum(parts), jnp.concatenate(parts, axis=1)
 
     def merge(h, oa, la, ma, stats, far_o):
         peaks, totals = [], []
@@ -410,34 +420,38 @@
     def mix(hs, width):
         qs = [jnp.concatenate([qown[:, cols(h)], qx[:, cols(h)]], axis=0) for h in hs]
         ks = [kv[h, 0, pl.ds(0, width)] for h in hs]
-        vs = [jnp.concatenate([kv[h, 1, pl.ds(0, width)], jnp.ones((width, HD), jnp.bfloat16)], axis=1) for h in hs]
+        vs = [kv[h, 1, pl.ds(0, width)] for h in hs]
         scores = [dot_t(q, k) for q, k in zip(qs, ks)]
         weights = []
         for s in scores:
-            mv, wv = softmax_part(s[:tok], see_v)
-            ma, wa = softmax_part(s[tok:, :span], see_a)
+            mv, lv, wv = softmax_part(s[:tok], see_v)
+            ma, la, wa = softmax_part(s[tok:, :span], see_a)
             if width > span:
                 wa = jnp.concatenate([wa, jnp.zeros((2 * aud, width - span), jnp.bfloat16)], axis=1)
-            weights.append((mv, ma[:aud], jnp.concatenate([wv, wa], axis=0)))
-        return [(mv, ma, jnp.dot(w, v, preferred_element_type=jnp.float32)) for (mv, ma, w), v in zip(weights, vs)]
+            weights.append((mv, lv, ma[:aud], la[:aud], jnp.concatenate([wv, wa], axis=0)))
+        return [(mv, lv, ma, la, jnp.dot(w, v, preferred_element_type=jnp.float32))
+                for (mv, lv, ma, la, w), v in zip(weights, vs)]
 
     def heads_full(hs):
         stats, far_o = far_back(hs)
         mixed = mix(hs, keys)
-        merged = [merge(h, o[tok:tok + aud, :HD], o[tok:tok + aud, HD:], ma, stats, f)
-                  for h, (_, ma, o), f in zip(hs, mixed, far_o)]
-        for h, (_, _, o), joined in zip(hs, mixed, merged):
-            attn[:, cols(h)] = o[:tok, :HD] / o[:tok, HD:]
+        merged = [merge(h, o[tok:tok + aud], la, ma, stats, f)
+                  for h, (_, _, ma, la, o), f in zip(hs, mixed, far_o)]
+        for h, (_, lv, _, _, o), joined in zip(hs, mixed, merged):
+            attn[:, cols(h)] = o[:tok] / lv
             aattn[:, cols(h)] = joined
 
     def heads_video(hs):
-        for h, (mv, ma, o) in zip(hs, mix(hs, span)):
-            attn[:, cols(h)] = o[:tok, :HD]
-            sums[h] = o[:tok, HD:]
+        for h, (mv, lv, ma, la, o) in zip(hs, mix(hs, span)):
+            attn[:, cols(h)] = o[:tok]
+            sums[h] = jnp.broadcast_to(lv, (tok, HD))
             tops[h] = jnp.broadcast_to(mv, (tok, HD))
-            aattn[:, cols(h)] = o[tok:tok + aud, :HD]
-            asums[h] = o[tok:tok + aud, HD:]
+            aattn[:, cols(h)] = o[tok:tok + aud]
+            asums[h] = jnp.broadcast_to(la, (aud, HD))
             atops[h] = jnp.broadcast_to(ma, (aud, HD))
+
+    def row_peak(peak, s):
+        return peak if peak.shape == s.shape else peak[:, :1]
 
     def heads_audio(hs):
         stats, far_o = far_back(hs)
@@ -449,7 +463,7 @@
         scores = [dot_t(q, k) * SCALE for q, k, _ in loaded]
         peaks = [jnp.maximum(jnp.max(s, axis=1, keepdims=True), top) for s, (_, _, top, _, _, _) in zip(scores, held)]
         mixed = [
-            jnp.dot(jnp.exp2(s - peak[:, :1]).astype(jnp.bfloat16), v, preferred_element_type=jnp.float32)
+            jnp.dot(jnp.exp2(s - row_peak(peak, s)).astype(jnp.bfloat16), v, preferred_element_type=jnp.float32)
             for s, peak, (_, _, v) in zip(scores, peaks, loaded)]
         merged = [merge(h, oa, la, ma, stats, f) for h, (_, _, _, oa, la, ma), f in zip(hs, held, far_o)]
         for h, o, peak, (old, total, top, _, _, _), joined in zip(hs, mixed, peaks, held, merged):
@@ -458,12 +472,8 @@
             aattn[:, cols(h)] = joined
 
     def far_sent():
-        for slot, exists, device in far:
-            @pl.when(exists)
-            def _(slot=slot, device=device):
-                q_copy(slot, device).wait_send()
-                bo_copy(slot, device).wait_send()
-                bs_copy(slot, device).wait_send()
+        for exist, copy in far_pairs(part_o, s_fo, 2) + far_pairs(part_s, s_bs):
+            pl.when(exist)(copy.wait_send)
 
     def audio_sent():
         several(chips, s_aud).wait_send()
@@ -479,12 +489,12 @@
     late = has_fwd & (behind >= 2)
 
     def z_due(i):
-        inner = i - LAG_Z + 1 + (edge & (i >= 9)).astype(jnp.int32)
-        return jnp.clip(jnp.where(has_src, inner, i + 1), 0, heads)
+        inner = (i - LAG_Z + 1 + (edge & (i == last - 1)).astype(jnp.int32)) // PAIR
+        return jnp.clip(jnp.where(has_src, inner, (i + 1) // PAIR), 0, pairs - 1)
 
     def v_due(i):
         inner = jnp.clip((i - LAG_Z) // PAIR, 0, MAIN_PAIRS)
-        return jnp.where(has_src, inner, jnp.clip(jnp.where(i < FAR_STEPS, 0, (i - 1) // PAIR), 0, pairs - 1))
+        return jnp.where(has_src, inner, jnp.clip(jnp.where(i < FAR_STEPS + FAR_FIRST, 0, (i - 1) // PAIR), 0, pairs - 1))
 
     def last_out():
         for p in range(LAST_PIECES):
@@ -499,23 +509,21 @@
             def _(p=p):
                 z_piece(h, p).start()
 
-    def take_z(k, _):
-        @pl.when(has_src & (k > 0) & (k < last))
+    def z_there(first, count, sem):
+        @pl.when(has_src)
         def _():
             with part("zwait"):
-                z_copy(k).wait_recv()
-
-        for h in (0, last):
-            @pl.when(has_src & (k == h))
-            def _(h=h):
-                with part("zwaitp"):
-                    for p in range(pieces(h)):
-                        z_piece(h, p).wait_recv()
-
-        @pl.when((k % PAIR == PAIR - 1) & jnp.logical_not(edge & (k == last)))
-        def _():
-            d_copy(k // PAIR).start()
+                there = kv.at[pl.ds(first, count), :, pl.ds(3 * tok, tok)]
+                remote(there, there, s_z, r_z.at[sem], fwd).wait_recv()
+
+    def take_z(p, _):
+        z_there(PAIR * p, PAIR, p)
+        d_copy(p).start()
         return 0
+
+    def take_last(share):
+        z_there(last - PAIR + share, 1, pairs - 2 + share)
+        d_last(share).start()
 
     def arrive(p):
         with part("dwait"):
@@ -538,11 +546,8 @@
         with part("layaudio"):
             lax.fori_loop(0, chips, lay_audio, 0)
         with part("bowait"):
-            for slot, exists, device in far:
-                @pl.when(exists)
-                def _(slot=slot):
-                    bo_copy(1 - slot, mate).wait_recv()
-                    bs_copy(1 - slot, mate).wait_recv()
+            for exist, copy in far_pairs(back_o, r_bo) + far_pairs(back_s, r_bs):
+                pl.when(exist)(copy.wait_recv)
 
     def relay(i, _):
         @pl.when((i > 0) & (i < last))
@@ -569,30 +574,31 @@
         @pl.when((i == last) & jnp.logical_not(edge))
         def _():
             take_y(last)
+            d_last(0).start()
 
         lax.fori_loop(z_due(i - 1), z_due(i), take_z, 0)
 
-        @pl.when(i == 0)
+        @pl.when(i == FAR_FIRST)
         def _():
             with part("faropen"):
                 far_open()
 
-        @pl.when(i < FAR_STEPS)
+        @pl.when((i >= FAR_FIRST) & (i < FAR_FIRST + FAR_STEPS))
         def _():
             with part("far"):
-                far_some(i)
-
-        @pl.when(i == FAR_STEPS - 1)
+                far_some(i - FAR_FIRST)
+
+        @pl.when(i == FAR_FIRST + FAR_STEPS - 1)
         def _():
             far_close()
 
-        for k, at in enumerate(WAVES[:-1]):
-            @pl.when(i == at)
+        for k, at in enumerate(zip(WAVES[:-1], WAVES_ALONE[:-1])):
+            @pl.when(i == jnp.where(has_src, *at))
             def _(k=k):
                 with part("wave"):
                     wave_step(k)
 
-        @pl.when(i == WAVES[-1])
+        @pl.when(i == jnp.where(has_src, WAVES[-1], WAVES_ALONE[-1]))
         def _():
             def more(k, _):
                 wave_step(k)
@@ -628,24 +634,32 @@
     def _():
         audio_in()
     lax.fori_loop(0, first_groups, attend_audio, 0)
-    lax.fori_loop(z_due(last), heads - 2, take_z, 0)
+    lax.fori_loop(z_due(last), pairs - 1, take_z, 0)
+    @pl.when(edge)
+    def _():
+        with part("passaudio"):
+            pass_audio()
     lax.fori_loop(v_due(last), pairs - 2, attend_video, 0)
-    with part("passaudio"):
-        pass_audio()
-    lax.fori_loop(jnp.maximum(z_due(last), heads - 2), last, take_z, 0)
+
+    @pl.when(late)
+    def _():
+        with part("passaudio"):
+            pass_audio()
     lax.fori_loop(jnp.maximum(v_due(last), pairs - 2), pairs - 1, attend_video, 0)
-    lax.fori_loop(jnp.maximum(z_due(last), last), heads, take_z, 0)
+    take_last(1)
+    take_last(2)
 
     @pl.when(edge)
     def _():
         take_y(last)
-        d_copy(pairs - 1).start()
+        d_last(0).start()
 
     @pl.when(jnp.logical_not(soon))
     def _():
         audio_in()
     lax.fori_loop(first_groups, groups, attend_audio, 0)
-    arrive(pairs - 1)
+    with part("dwait"):
+        d_copy(pairs - 1).wait_recv()
     with part("head"):
         heads_full([PAIR * (pairs - 1) + k for k in range(PAIR)])
 
@@ -660,13 +674,23 @@
             remote(z_sent, z_sent, s_z, r_dk, mate).wait_send()
 
 
-def finish_kernel(attn, aattn, vgain, again, vout, aout):
+def finish_kernel(attn, aattn, vgain, again, vout, aout, vbuf, abuf, sems):
     def finish(mixed, gain):
         scale = lax.rsqrt(jnp.mean(mixed * mixed, axis=1, keepdims=True) + EPS)
         return (mixed * scale * gain[...].reshape(1, mixed.shape[1])).astype(jnp.bfloat16)
 
-    vout[...] = finish(attn[...], vgain)
-    aout[...] = finish(aattn[...], again)
+    rows = vbuf.shape[0] // OUT_PIECES
+    copies = []
+    for p in range(OUT_PIECES):
+        at = pl.ds(p * rows, rows)
+        vbuf[at, :] = finish(attn[at, :], vgain)
+        copies.append(pltpu.make_async_copy(vbuf.at[at], vout.at[at], sems.at[p]))
+        copies[-1].start()
+    abuf[...] = finish(aattn[...], again)
+    copies.append(pltpu.make_async_copy(abuf, aout, sems.at[OUT_PIECES]))
+    copies[-1].start()
+    for copy in copies:
+        copy.wait()
 
 
 def solution(mesh):
@@ -702,16 +726,16 @@
                 pltpu.VMEM((2, aud, width), bf),
                 pltpu.VMEM((2 * aud, width), bf),
                 pltpu.VMEM((2 * aud, width), bf),
-                pltpu.VMEM((2, aud, width), bf),
+                pltpu.VMEM((4, aud, width), bf),
                 pltpu.VMEM((2, aud, HD), f32),
                 pltpu.VMEM((2, aud, width), bf),
                 pltpu.VMEM((2, aud, HD), f32),
                 *([pltpu.VMEM((heads, tok, HD), f32)] * 2),
                 *([pltpu.VMEM((heads, aud, HD), f32)] * 2),
                 dma((8,)), dma((OWN_FIRST + 1,)), dma, dma,
-                dma((heads - 2 + FIRST_PIECES + LAST_PIECES,)), dma, dma((heads - 2 + FIRST_PIECES + LAST_PIECES,)), dma((heads // PAIR,)),
-                dma, dma((chips,)), dma, dma,
-                *([dma((2,))] * 6),
+                dma((heads - 2 + FIRST_PIECES + LAST_PIECES,)), dma, dma((heads // PAIR + 1,)), dma((heads // PAIR,)),
+                dma, dma((chips // 2,)), dma, dma,
+                *([dma] * 5),
             ],
             compiler_params=pltpu.CompilerParams(
                 collective_id=0, has_side_effects=True),
@@ -720,7 +744,8 @@
             finish_kernel,
             out_shape=(jax.ShapeDtypeStruct(vq.shape, bf), jax.ShapeDtypeStruct(aq.shape, bf)),
             in_specs=[vmem] * 4,
-            out_specs=(vmem, vmem),
+            out_specs=(hbm, hbm),
+            scratch_shapes=[pltpu.VMEM(vq.shape, bf), pltpu.VMEM(aq.shape, bf), dma((OUT_PIECES + 1,))],
             compiler_params=pltpu.CompilerParams(vmem_limit_bytes=8 * 1024 * 1024),
         )(*mixed)
 

time: 31.5 us -> 30.9 us (0.981); the launches traced: 31.4 us -> 30.4 us
  Pallas kernels: 30.1 us -> 29.1 us
    pallas_call x1, Pallas kernels: 29.2 us -> 28.2 us  [on_device(): pl.pallas_call(functools.partial(kernel, n, heads, tok, aud, tile_list.sh...]
where the time goes in v3:
time: 30.9 us; the launch traced here: 30.4 us
  Pallas kernels  29.1 us (94%)
  between operations  1.29 us (4%)
    pallas_call x1, Pallas kernels, on_device(): pl.pallas_call(functools.partial(kernel, n, heads, tok, aud, tile_list.sh...  28.2 us
    pallas_call x1, Pallas kernels, on_device(): pl.pallas_call(finish_kernel, out_shape=(jax.ShapeDtypeStruct(vq.shape, b...  0.9 us

profile of v3, /device:TPU:5, one launch (start us, length us, event | category | flops | bytes accessed | tf_op | source)
XLA Modules:
  0.0 30.4 jit_solution(4245948149503129825)
XLA Ops:
  1.3 28.2 %shard_map.122 = (f32[128,1536]{1,0:T(8,128)S(1)}, f32[8,1536]{1,0:T(8,128)S(1)}, f32[1536]{0:T(1024)S(1)}, f32[1536]{0:T(1024)S(1)}) custom-call(s32[1]{0:T(128)S(6)} %copy.13.radius_hbm, s32[5,16]{1,0:T(8,128)} %bitcast.1, s32[16]{0:T(128)} %tile_count_hbm.1, bf16[128,1536]{1,0:T(8,128)(2,1)} %vq_hbm.1, bf16[128,1536]{1,0:T(8,128)(2,1)} %vk_hbm.1, ...), custom_call_target="tpu_custom_call" | custom-call | tf_op jit(solution)/shard_map/pallas_call | solution.py:710
  29.4 0.9 %shard_map.123 = (bf16[128,1536]{1,0:T(8,128)(2,1)}, bf16[8,1536]{1,0:T(8,128)(2,1)}) custom-call(f32[128,1536]{1,0:T(8,128)S(1)} %get-tuple-element.6.attn, f32[8,1536]{1,0:T(8,128)S(1)} %get-tuple-element.7.aattn, f32[1536]{0:T(1024)S(1)} %get-tuple-element.8.vgain, f32[1536]{0:T(1024)S(1)} %get-tuple-element.9.again), custom_call_target="tpu_custom_call" | custom-call | tf_op jit(solution)/shard_map/pallas_call | solution.py:743
